TPU v7x, 32 devices: a whole 2x2x4 slice. The times are simulated.
32 devices in a mesh: gx: 2 (over x), gy: 4 (over y, core), gz: 4 (over z).
Axes of the slice: x: 2, y: 2, z: 4, core: 2. Of those that a mesh axis runs over, the one named last changes fastest.
Arguments:
- velocity: float32 [3, 32, 64, 1024], P(None, 'gx', 'gy', 'gz'), may hold values from -24 to 24
- metric: float32 [3, 32, 64, 1024], P(None, 'gx', 'gy', 'gz'), may hold values from 0.5 to 2
Outputs:
- viscosity: float32 [32, 64, 1024], P('gx', 'gy', 'gz')
- coefficient: float32 [32, 64], P('gx', 'gy')
All inputs are finite; a program needn't handle non-finite values.
Results may differ from a plain program's by a relative error of at most 0.0003.
Values sent between devices are 32-bit elements; how exact they have to be, the bound alone decides.
A program may use at most 64 MiB of HBM per device.

v0:
```python
import jax
import jax.numpy as jnp
from jax import lax
from jax.sharding import PartitionSpec as P

pair_rows = (0, 1, 2, 0, 0, 1)
pair_cols = (0, 1, 2, 1, 2, 2)
pair_weight = (1.0, 1.0, 1.0, 2.0, 2.0, 2.0)
eps_line = 1e-06
ratio_square = 4.0


def with_halo(block, sides, width, periodic):
    for axis, dim in sides:
        count = lax.axis_size(axis)
        forward = [(i, i + 1) for i in range(count - 1)]
        if periodic:
            forward.append((count - 1, 0))
        backward = [(target, source) for source, target in forward]
        low = lax.ppermute(
            lax.slice_in_dim(block, block.shape[dim] - width, None, axis=dim), axis, forward
        )
        high = lax.ppermute(lax.slice_in_dim(block, 0, width, axis=dim), axis, backward)
        block = jnp.concatenate([low, block, high], axis=dim)
    return block


def box_three(padded, axis_pos):
    length_axis = padded.shape[axis_pos]
    lower_side = lax.slice_in_dim(padded, 0, length_axis - 2, axis=axis_pos)
    middle = lax.slice_in_dim(padded, 1, length_axis - 1, axis=axis_pos)
    upper_side = lax.slice_in_dim(padded, 2, length_axis, axis=axis_pos)
    return 0.25 * lower_side + 0.5 * middle + 0.25 * upper_side


def gradient_field(velocity_part, metric):
    around_span = with_halo(velocity_part, (("gz", 3),), 1, True)
    around_plane = with_halo(velocity_part, (("gx", 1), ("gy", 2)), 1, False)
    diff_chord = around_plane[:, 2:, 1:-1, :] - around_plane[:, :-2, 1:-1, :]
    diff_normal = around_plane[:, 1:-1, 2:, :] - around_plane[:, 1:-1, :-2, :]
    diff_span = around_span[:, :, :, 2:] - around_span[:, :, :, :-2]
    return jnp.stack(
        [0.5 * metric[0] * diff_chord, 0.5 * metric[1] * diff_normal, 0.5 * metric[2] * diff_span],
        axis=1,
    )


def strain_parts(gradients):
    strain = 0.5 * (gradients + jnp.swapaxes(gradients, 0, 1))
    magnitude = jnp.sqrt(2.0 * jnp.sum(strain * strain, axis=(0, 1)))
    strain_pairs = jnp.stack(
        [strain[row_index, col_index] for row_index, col_index in zip(pair_rows, pair_cols)]
    )
    return (strain_pairs, magnitude)


def make_fields(velocity_part, strain_pairs, magnitude):
    products = jnp.stack(
        [
            velocity_part[row_index] * velocity_part[col_index]
            for row_index, col_index in zip(pair_rows, pair_cols)
        ]
    )
    return jnp.concatenate([velocity_part, products, magnitude[None] * strain_pairs], axis=0)


def germano(filtered, strain_hat, magnitude_hat, delta_sq):
    numerator = jnp.zeros_like(delta_sq)
    denominator = jnp.zeros_like(delta_sq)
    for position in range(6):
        row_index = pair_rows[position]
        col_index = pair_cols[position]
        leonard = filtered[3 + position] - filtered[row_index] * filtered[col_index]
        model_term = (
            2.0
            * delta_sq
            * (filtered[9 + position] - ratio_square * magnitude_hat * strain_hat[position])
        )
        numerator = numerator + pair_weight[position] * leonard * model_term
        denominator = denominator + pair_weight[position] * model_term * model_term
    return (numerator, denominator)


def per_device(velocity, metric):
    delta_sq = (metric[0] * metric[1] * metric[2]) ** (-2.0 / 3.0)
    strain_pairs, magnitude = strain_parts(gradient_field(velocity, metric))
    fields = make_fields(velocity, strain_pairs, magnitude)
    span_done = box_three(with_halo(fields, (("gz", 3),), 1, True), 3)
    chord_done = box_three(with_halo(span_done, (("gx", 1),), 1, False), 1)
    filtered = box_three(with_halo(chord_done, (("gy", 2),), 1, False), 2)
    strain_hat, magnitude_hat = strain_parts(gradient_field(filtered[0:3], metric))
    numerator, denominator = germano(filtered, strain_hat, magnitude_hat, delta_sq)
    span_cells = numerator.shape[2] * lax.axis_size("gz")
    num_part = jnp.sum(numerator, axis=2)
    den_part = jnp.sum(denominator, axis=2)
    line_num, line_den = lax.psum((num_part, den_part), "gz")
    line_coef = line_num / span_cells / (line_den / span_cells + eps_line)
    peak_coef = lax.pmax(jnp.max(line_coef), ("gx", "gy"))
    coefficient = jnp.minimum(line_coef, 0.5 * peak_coef)
    viscosity = coefficient[:, :, None] * delta_sq * magnitude
    return (viscosity, coefficient)


def solution(mesh):
    return jax.shard_map(
        per_device,
        mesh=mesh,
        in_specs=(P(None, "gx", "gy", "gz"), P(None, "gx", "gy", "gz")),
        out_specs=(P("gx", "gy", "gz"), P("gx", "gy")),
        check_vma=False,
    )
```

profile of v0, /device:TPU:0, one launch (start us, length us, event | category | flops | bytes accessed | tf_op | source)
XLA Modules:
  0.0 159.2 jit_solution(4024250551221104019)
XLA Ops:
  0.6 0.9 fusion.88
  1.5 4.9 %collective-permute-start.1 = (f32[3,1,16,256]{3,2,1,0:T(8,128)S(1)}, f32[3,1,16,256]{3,2,1,0:T(8,128)S(1)}, u32[]{:S(2)}, u32[]{:S(2)}) collective-permute-start(f32[3,1,16,256]{3,2,1,0:T(8,128)S(1)} %get-tuple-element.44), channel_id=1, source_target_pairs={{0,16},{1,17},{2,18},{3,19},{4,20},{5,21},{6,22},{7,23},{8,24},{9,... | collective-permute-start | bytes 147464 | tf_op jit(solution)/shard_map/ppermute | solution.py:20
  6.4 1.3 collective-permute-start
  7.7 1.3 fusion.89
  9.0 3.7 %collective-permute-start.4 = (f32[3,16,16,1]{3,2,1,0:T(8,128)S(1)}, f32[3,16,16,1]{3,2,1,0:T(8,128)S(1)}, u32[]{:S(2)}, u32[]{:S(2)}) collective-permute-start(f32[3,16,16,1]{3,2,1,0:T(8,128)S(1)} %get-tuple-element.45), channel_id=1, source_target_pairs={{1,0},{2,1},{3,2},{0,3},{5,4},{6,5},{7,6},{4,7},{9,8},{10,9},{11,1... | collective-permute-start | bytes 9224 | tf_op jit(solution)/shard_map/ppermute | solution.py:23
  12.7 1.2 multiply_bitcast_fusion.2
  13.9 8.3 %collective-permute-done.4 = f32[3,16,16,1]{3,2,1,0:T(8,128)S(1)} collective-permute-done((f32[3,16,16,1]{3,2,1,0:T(8,128)S(1)}, f32[3,16,16,1]{3,2,1,0:T(8,128)S(1)}, u32[]{:S(2)}, u32[]{:S(2)}) %collective-permute-start.4) | collective-permute-done | bytes 3104 | tf_op jit(solution)/shard_map/ppermute | solution.py:23
  22.2 7.9 %collective-permute-done.5 = f32[3,16,16,1]{3,2,1,0:T(8,128)S(1)} collective-permute-done((f32[3,16,16,1]{3,2,1,0:T(8,128)S(1)}, f32[3,16,16,1]{3,2,1,0:T(8,128)S(1)}, u32[]{:S(2)}, u32[]{:S(2)}) %collective-permute-start.5) | collective-permute-done | bytes 3104 | tf_op jit(solution)/shard_map/ppermute | solution.py:20
  30.1 0.8 fusion.30
  30.9 0.1 fusion.87
  31.0 1.3 collective-permute-start.2
  32.3 3.0 %collective-permute-start.3 = (f32[3,18,1,256]{3,2,1,0:T(1,128)S(1)}, f32[3,18,1,256]{3,2,1,0:T(1,128)S(1)}, u32[]{:S(2)}, u32[]{:S(2)}) collective-permute-start(f32[3,18,1,256]{3,2,1,0:T(1,128)S(1)} %get-tuple-element.34), channel_id=1, source_target_pairs={{0,4},{4,8},{8,12},{1,5},{5,9},{9,13},{2,6},{6,10},{10,14},{3,7},{... | collective-permute-start | bytes 165896 | tf_op jit(solution)/shard_map/ppermute | solution.py:20
  35.5 0.7 collective-permute-done.3
  36.2 0.3 fusion.27
  36.5 0.2 pad_maximum_fusion.6
  36.7 0.4 multiply_reduce_fusion.1
  37.2 0.1 multiply_sqrt_fusion
  37.3 0.1 fusion.74
  37.4 0.2 multiply_dynamic-update-slice_fusion
  37.6 1.8 %copy-done.1 = f32[15,16,16,256]{3,2,1,0:T(8,128)} copy-done((f32[15,16,16,256]{3,2,1,0:T(8,128)}, f32[15,16,16,256]{3,2,1,0:T(8,128)S(1)}, u32[]{:S(2)}) %copy-start.1) | copy-done | bytes 3932184
  39.4 2.0 %fusion.86 = (f32[15,16,16,1]{3,2,1,0:T(8,128)}, f32[15,16,16,1]{3,2,1,0:T(8,128)S(1)}) fusion(f32[15,16,16,256]{3,2,1,0:T(8,128)S(1)} %multiply_dynamic-update-slice_fusion), kind=kLoop, calls=%fused_computation.166 | loop fusion | bytes 61440 | tf_op jit(solution)/shard_map/slice | solution.py:21
  41.4 3.0 %copy.94 = f32[15,16,16,1]{2,1,3,0:T(8,128)S(1)} copy(f32[15,16,16,1]{3,2,1,0:T(8,128)} %get-tuple-element.23) | data formatting | bytes 30720
  44.4 1.7 %collective-permute-start.6 = (f32[15,16,16,1]{2,1,3,0:T(8,128)S(1)}, f32[15,16,16,1]{2,1,3,0:T(8,128)S(1)}, u32[]{:S(2)}, u32[]{:S(2)}) collective-permute-start(f32[15,16,16,1]{2,1,3,0:T(8,128)S(1)} %copy.94), channel_id=1, source_target_pairs={{0,1},{1,2},{2,3},{3,0},{4,5},{5,6},{6,7},{7,4},{8,9},{9,10},{10,1... | collective-permute-start | bytes 46088 | tf_op jit(solution)/shard_map/ppermute | solution.py:20
  46.1 1.5 copy.95
  47.5 2.2 %collective-permute-start.7 = (f32[15,16,16,1]{2,1,3,0:T(8,128)S(1)}, f32[15,16,16,1]{2,1,3,0:T(8,128)S(1)}, u32[]{:S(2)}, u32[]{:S(2)}) collective-permute-start(f32[15,16,16,1]{2,1,3,0:T(8,128)S(1)} %copy.95), channel_id=1, source_target_pairs={{1,0},{2,1},{3,2},{0,3},{5,4},{6,5},{7,6},{4,7},{9,8},{10,9},{11,1... | collective-permute-start | bytes 46088 | tf_op jit(solution)/shard_map/ppermute | solution.py:23
  49.8 2.3 %collective-permute-done.6 = f32[15,16,16,1]{2,1,3,0:T(8,128)S(1)} collective-permute-done((f32[15,16,16,1]{2,1,3,0:T(8,128)S(1)}, f32[15,16,16,1]{2,1,3,0:T(8,128)S(1)}, u32[]{:S(2)}, u32[]{:S(2)}) %collective-permute-start.6) | collective-permute-done | bytes 15392 | tf_op jit(solution)/shard_map/ppermute | solution.py:20
  52.1 1.5 copy.85
  53.5 1.5 collective-permute-done.7
  55.0 2.8 %copy.87 = f32[15,16,16,1]{3,2,1,0:T(8,128)} copy(f32[15,16,16,1]{2,1,3,0:T(8,128)S(1)} %collective-permute-done.7) | data formatting | bytes 30720 | tf_op jit(solution)/shard_map/ppermute | solution.py:23
  57.8 6.7 %fusion.9 = f32[15,16,16,256]{3,2,1,0:T(8,128)S(1)} fusion(f32[15,16,16,1]{3,2,1,0:T(8,128)} %copy.87, f32[15,16,16,256]{3,2,1,0:T(8,128)} %copy-done.1, f32[15,16,16,1]{3,2,1,0:T(8,128)S(1)} %copy.85), kind=kLoop, calls=%fused_computation.14 | loop fusion | flops 6881280 | bytes 7895040 | tf_op jit(solution)/shard_map/add | solution.py:33
  64.5 4.3 %collective-permute-start.8 = (f32[15,1,16,256]{3,2,1,0:T(8,128)S(1)}, f32[15,1,16,256]{3,2,1,0:T(8,128)S(1)}, u32[]{:S(2)}, u32[]{:S(2)}) collective-permute-start(f32[15,1,16,256]{3,2,1,0:T(8,128)S(1)} %get-tuple-element.21), channel_id=1, source_target_pairs={{0,16},{1,17},{2,18},{3,19},{4,20},{5,21},{6,22},{7,23},{8,24},{9,... | collective-permute-start | bytes 737288 | tf_op jit(solution)/shard_map/ppermute | solution.py:20
  68.8 1.3 collective-permute-start.9
  70.1 4.2 %collective-permute-done.8 = f32[15,1,16,256]{3,2,1,0:T(8,128)S(1)} collective-permute-done((f32[15,1,16,256]{3,2,1,0:T(8,128)S(1)}, f32[15,1,16,256]{3,2,1,0:T(8,128)S(1)}, u32[]{:S(2)}, u32[]{:S(2)}) %collective-permute-start.8) | collective-permute-done | bytes 245792 | tf_op jit(solution)/shard_map/ppermute | solution.py:20
  74.3 4.1 %collective-permute-done.9 = f32[15,1,16,256]{3,2,1,0:T(8,128)S(1)} collective-permute-done((f32[15,1,16,256]{3,2,1,0:T(8,128)S(1)}, f32[15,1,16,256]{3,2,1,0:T(8,128)S(1)}, u32[]{:S(2)}, u32[]{:S(2)}) %collective-permute-start.9) | collective-permute-done | bytes 245792 | tf_op jit(solution)/shard_map/ppermute | solution.py:23
  78.4 0.9 fusion.5
  79.3 0.5 fusion.84
  79.9 1.3 collective-permute-start.10
  81.2 1.3 collective-permute-start.11
  82.5 0.3 copy.89
  82.8 2.0 %collective-permute-done.11 = f32[15,16,1,256]{3,1,2,0:T(8,128)S(1)} collective-permute-done((f32[15,16,1,256]{3,1,2,0:T(8,128)S(1)}, f32[15,16,1,256]{3,1,2,0:T(8,128)S(1)}, u32[]{:S(2)}, u32[]{:S(2)}) %collective-permute-start.11) | collective-permute-done | bytes 245792 | tf_op jit(solution)/shard_map/ppermute | solution.py:23
  84.8 0.3 copy.91
  85.1 2.0 %fusion.1 = f32[15,16,16,256]{3,2,1,0:T(8,128)S(1)} fusion(f32[15,16,1,256]{3,2,1,0:T(1,128)S(1)} %copy.91, f32[15,16,16,256]{3,2,1,0:T(8,128)S(1)} %fusion.5, f32[15,16,1,256]{3,2,1,0:T(1,128)S(1)} %copy.89), kind=kLoop, calls=%fused_computation.2 | loop fusion | flops 6881280 | bytes 8355840 | tf_op jit(solution)/shard_map/add | solution.py:33
  87.1 1.3 collective-permute-start.12
  88.4 4.5 %collective-permute-start.13 = (f32[3,1,16,256]{3,2,1,0:T(8,128)S(1)}, f32[3,1,16,256]{3,2,1,0:T(8,128)S(1)}, u32[]{:S(2)}, u32[]{:S(2)}) collective-permute-start(f32[3,1,16,256]{3,2,1,0:T(8,128)S(1)} %get-tuple-element.15), channel_id=1, source_target_pairs={{0,16},{1,17},{2,18},{3,19},{4,20},{5,21},{6,22},{7,23},{8,24},{9,... | collective-permute-start | bytes 147464 | tf_op jit(solution)/shard_map/ppermute | solution.py:20
  93.0 0.1 collective-permute-done.12
  93.1 1.6 %collective-permute-done.13 = f32[3,1,16,256]{3,2,1,0:T(8,128)S(1)} collective-permute-done((f32[3,1,16,256]{3,2,1,0:T(8,128)S(1)}, f32[3,1,16,256]{3,2,1,0:T(8,128)S(1)}, u32[]{:S(2)}, u32[]{:S(2)}) %collective-permute-start.13) | collective-permute-done | bytes 49184 | tf_op jit(solution)/shard_map/ppermute | solution.py:20
  94.7 0.1 pad_maximum_fusion.26
  94.8 1.3 collective-permute-start.14
  96.1 6.0 %collective-permute-start.15 = (f32[3,18,1,256]{3,2,1,0:T(1,128)S(1)}, f32[3,18,1,256]{3,2,1,0:T(1,128)S(1)}, u32[]{:S(2)}, u32[]{:S(2)}) collective-permute-start(f32[3,18,1,256]{3,2,1,0:T(1,128)S(1)} %get-tuple-element.32), channel_id=1, source_target_pairs={{0,4},{4,8},{8,12},{1,5},{5,9},{9,13},{2,6},{6,10},{10,14},{3,7},{... | collective-permute-start | bytes 165896 | tf_op jit(solution)/shard_map/ppermute | solution.py:20
  102.1 0.2 fusion.83
  102.3 3.7 %collective-permute-start.16 = (f32[3,16,16,1]{3,2,1,0:T(8,128)S(1)}, f32[3,16,16,1]{3,2,1,0:T(8,128)S(1)}, u32[]{:S(2)}, u32[]{:S(2)}) collective-permute-start(f32[3,16,16,1]{3,2,1,0:T(8,128)S(1)} %get-tuple-element.17), channel_id=1, source_target_pairs={{1,0},{2,1},{3,2},{0,3},{5,4},{6,5},{7,6},{4,7},{9,8},{10,9},{11,1... | collective-permute-start | bytes 9224 | tf_op jit(solution)/shard_map/ppermute | solution.py:23
  106.0 8.8 %collective-permute-done.16 = f32[3,16,16,1]{3,2,1,0:T(8,128)S(1)} collective-permute-done((f32[3,16,16,1]{3,2,1,0:T(8,128)S(1)}, f32[3,16,16,1]{3,2,1,0:T(8,128)S(1)}, u32[]{:S(2)}, u32[]{:S(2)}) %collective-permute-start.16) | collective-permute-done | bytes 3104 | tf_op jit(solution)/shard_map/ppermute | solution.py:23
  114.8 8.6 %collective-permute-done.17 = f32[3,16,16,1]{3,2,1,0:T(8,128)S(1)} collective-permute-done((f32[3,16,16,1]{3,2,1,0:T(8,128)S(1)}, f32[3,16,16,1]{3,2,1,0:T(8,128)S(1)}, u32[]{:S(2)}, u32[]{:S(2)}) %collective-permute-start.17) | collective-permute-done | bytes 3104 | tf_op jit(solution)/shard_map/ppermute | solution.py:20
  123.4 0.8 fusion.21
  124.2 0.2 pad_maximum_fusion.7
  124.4 0.5 multiply_reduce_fusion
  124.9 0.4 copy-done.2
  125.3 0.4 fusion.71
  125.7 0.4 fusion.65
  126.1 0.6 fusion.42
  126.7 18.0 %all-reduce = (f32[16,16]{1,0:T(8,128)S(1)}, f32[16,16]{1,0:T(8,128)S(1)}) all-reduce(f32[16,16]{1,0:T(8,128)S(1)} %get-tuple-element.5, f32[16,16]{1,0:T(8,128)S(1)} %get-tuple-element.4), channel_id=1, replica_groups=mesh['gx'=2,'gy'=4,'gz'=4] {'gz'}, use_global_device_ids=true, to_apply=%region_5.0 | all-reduce | flops 512 | bytes 4096 | tf_op jit(solution)/shard_map/psum | solution.py:96
  144.6 0.6 fusion.81
  145.2 12.4 %pmax.7 = f32[]{:T(128)} all-reduce(f32[]{:T(128)} %fusion.81), channel_id=1, replica_groups=mesh['gx'=2,'gy'=4,'gz'=4] {'gx','gy'}, use_global_device_ids=true, to_apply=%region_7.0 | all-reduce | flops 1 | bytes 8 | tf_op jit(solution)/shard_map/pmax | solution.py:98
  158.3 0.9 fusion.80
  (32 shorter events, 0.4 us)
Async XLA Ops:
  0.6 29.5 %copy-start = (f32[3,16,16,256]{3,2,1,0:T(8,128)S(1)}, f32[3,16,16,256]{3,2,1,0:T(8,128)}, u32[]{:S(2)}) copy-start(f32[3,16,16,256]{3,2,1,0:T(8,128)} %param.2) | copy-start | bytes 2359300
  1.5 12.3 %collective-permute-start.1 = (f32[3,1,16,256]{3,2,1,0:T(8,128)S(1)}, f32[3,1,16,256]{3,2,1,0:T(8,128)S(1)}, u32[]{:S(2)}, u32[]{:S(2)}) collective-permute-start(f32[3,1,16,256]{3,2,1,0:T(8,128)S(1)} %get-tuple-element.44), channel_id=1, source_target_pairs={{0,16},{1,17},{2,18},{3,19},{4,20},{5,21},{6,22},{7,23},{8,24},{9,... | collective-permute-start | bytes 147464 | tf_op jit(solution)/shard_map/ppermute | solution.py:20
  6.4 23.7 %collective-permute-start = (f32[3,1,16,256]{3,2,1,0:T(8,128)S(1)}, f32[3,1,16,256]{3,2,1,0:T(8,128)S(1)}, u32[]{:S(2)}, u32[]{:S(2)}) collective-permute-start(f32[3,1,16,256]{3,2,1,0:T(8,128)S(1)} %get-tuple-element.43), channel_id=1, source_target_pairs={{16,0},{17,1},{18,2},{19,3},{20,4},{21,5},{22,6},{23,7},{24,8},{25... | collective-permute-start | bytes 147464 | tf_op jit(solution)/shard_map/ppermute | solution.py:23
  9.0 13.2 %collective-permute-start.4 = (f32[3,16,16,1]{3,2,1,0:T(8,128)S(1)}, f32[3,16,16,1]{3,2,1,0:T(8,128)S(1)}, u32[]{:S(2)}, u32[]{:S(2)}) collective-permute-start(f32[3,16,16,1]{3,2,1,0:T(8,128)S(1)} %get-tuple-element.45), channel_id=1, source_target_pairs={{1,0},{2,1},{3,2},{0,3},{5,4},{6,5},{7,6},{4,7},{9,8},{10,9},{11,1... | collective-permute-start | bytes 9224 | tf_op jit(solution)/shard_map/ppermute | solution.py:23
  12.7 17.4 %collective-permute-start.5 = (f32[3,16,16,1]{3,2,1,0:T(8,128)S(1)}, f32[3,16,16,1]{3,2,1,0:T(8,128)S(1)}, u32[]{:S(2)}, u32[]{:S(2)}) collective-permute-start(f32[3,16,16,1]{3,2,1,0:T(8,128)S(1)} %get-tuple-element.46), channel_id=1, source_target_pairs={{0,1},{1,2},{2,3},{3,0},{4,5},{5,6},{6,7},{7,4},{8,9},{9,10},{10,1... | collective-permute-start | bytes 9224 | tf_op jit(solution)/shard_map/ppermute | solution.py:20
  31.0 4.5 %collective-permute-start.2 = (f32[3,18,1,256]{3,2,1,0:T(1,128)S(1)}, f32[3,18,1,256]{3,2,1,0:T(1,128)S(1)}, u32[]{:S(2)}, u32[]{:S(2)}) collective-permute-start(f32[3,18,1,256]{3,2,1,0:T(1,128)S(1)} %get-tuple-element.33), channel_id=1, source_target_pairs={{4,0},{8,4},{12,8},{5,1},{9,5},{13,9},{6,2},{10,6},{14,10},{7,3},{... | collective-permute-start | bytes 165896 | tf_op jit(solution)/shard_map/ppermute | solution.py:23
  32.3 3.9 %collective-permute-start.3 = (f32[3,18,1,256]{3,2,1,0:T(1,128)S(1)}, f32[3,18,1,256]{3,2,1,0:T(1,128)S(1)}, u32[]{:S(2)}, u32[]{:S(2)}) collective-permute-start(f32[3,18,1,256]{3,2,1,0:T(1,128)S(1)} %get-tuple-element.34), channel_id=1, source_target_pairs={{0,4},{4,8},{8,12},{1,5},{5,9},{9,13},{2,6},{6,10},{10,14},{3,7},{... | collective-permute-start | bytes 165896 | tf_op jit(solution)/shard_map/ppermute | solution.py:20
  37.6 1.9 %copy-start.1 = (f32[15,16,16,256]{3,2,1,0:T(8,128)}, f32[15,16,16,256]{3,2,1,0:T(8,128)S(1)}, u32[]{:S(2)}) copy-start(f32[15,16,16,256]{3,2,1,0:T(8,128)S(1)} %multiply_dynamic-update-slice_fusion) | copy-start | bytes 11796484
  44.4 7.7 %collective-permute-start.6 = (f32[15,16,16,1]{2,1,3,0:T(8,128)S(1)}, f32[15,16,16,1]{2,1,3,0:T(8,128)S(1)}, u32[]{:S(2)}, u32[]{:S(2)}) collective-permute-start(f32[15,16,16,1]{2,1,3,0:T(8,128)S(1)} %copy.94), channel_id=1, source_target_pairs={{0,1},{1,2},{2,3},{3,0},{4,5},{5,6},{6,7},{7,4},{8,9},{9,10},{10,1... | collective-permute-start | bytes 46088 | tf_op jit(solution)/shard_map/ppermute | solution.py:20
  47.5 7.5 %collective-permute-start.7 = (f32[15,16,16,1]{2,1,3,0:T(8,128)S(1)}, f32[15,16,16,1]{2,1,3,0:T(8,128)S(1)}, u32[]{:S(2)}, u32[]{:S(2)}) collective-permute-start(f32[15,16,16,1]{2,1,3,0:T(8,128)S(1)} %copy.95), channel_id=1, source_target_pairs={{1,0},{2,1},{3,2},{0,3},{5,4},{6,5},{7,6},{4,7},{9,8},{10,9},{11,1... | collective-permute-start | bytes 46088 | tf_op jit(solution)/shard_map/ppermute | solution.py:23
  64.5 9.7 %collective-permute-start.8 = (f32[15,1,16,256]{3,2,1,0:T(8,128)S(1)}, f32[15,1,16,256]{3,2,1,0:T(8,128)S(1)}, u32[]{:S(2)}, u32[]{:S(2)}) collective-permute-start(f32[15,1,16,256]{3,2,1,0:T(8,128)S(1)} %get-tuple-element.21), channel_id=1, source_target_pairs={{0,16},{1,17},{2,18},{3,19},{4,20},{5,21},{6,22},{7,23},{8,24},{9,... | collective-permute-start | bytes 737288 | tf_op jit(solution)/shard_map/ppermute | solution.py:20
  68.8 9.6 %collective-permute-start.9 = (f32[15,1,16,256]{3,2,1,0:T(8,128)S(1)}, f32[15,1,16,256]{3,2,1,0:T(8,128)S(1)}, u32[]{:S(2)}, u32[]{:S(2)}) collective-permute-start(f32[15,1,16,256]{3,2,1,0:T(8,128)S(1)} %get-tuple-element.22), channel_id=1, source_target_pairs={{16,0},{17,1},{18,2},{19,3},{20,4},{21,5},{22,6},{23,7},{24,8},{25... | collective-permute-start | bytes 737288 | tf_op jit(solution)/shard_map/ppermute | solution.py:23
  79.9 2.6 %collective-permute-start.10 = (f32[15,16,1,256]{3,1,2,0:T(8,128)S(1)}, f32[15,16,1,256]{3,1,2,0:T(8,128)S(1)}, u32[]{:S(2)}, u32[]{:S(2)}) collective-permute-start(f32[15,16,1,256]{3,1,2,0:T(8,128)S(1)} %copy.88), channel_id=1, source_target_pairs={{0,4},{4,8},{8,12},{1,5},{5,9},{9,13},{2,6},{6,10},{10,14},{3,7},{... | collective-permute-start | bytes 737288 | tf_op jit(solution)/shard_map/ppermute | solution.py:20
  81.2 3.6 %collective-permute-start.11 = (f32[15,16,1,256]{3,1,2,0:T(8,128)S(1)}, f32[15,16,1,256]{3,1,2,0:T(8,128)S(1)}, u32[]{:S(2)}, u32[]{:S(2)}) collective-permute-start(f32[15,16,1,256]{3,1,2,0:T(8,128)S(1)} %copy.90), channel_id=1, source_target_pairs={{4,0},{8,4},{12,8},{5,1},{9,5},{13,9},{6,2},{10,6},{14,10},{7,3},{... | collective-permute-start | bytes 737288 | tf_op jit(solution)/shard_map/ppermute | solution.py:23
  87.1 6.0 %collective-permute-start.12 = (f32[3,1,16,256]{3,2,1,0:T(8,128)S(1)}, f32[3,1,16,256]{3,2,1,0:T(8,128)S(1)}, u32[]{:S(2)}, u32[]{:S(2)}) collective-permute-start(f32[3,1,16,256]{3,2,1,0:T(8,128)S(1)} %get-tuple-element.16), channel_id=1, source_target_pairs={{16,0},{17,1},{18,2},{19,3},{20,4},{21,5},{22,6},{23,7},{24,8},{25... | collective-permute-start | bytes 147464 | tf_op jit(solution)/shard_map/ppermute | solution.py:23
  88.4 6.3 %collective-permute-start.13 = (f32[3,1,16,256]{3,2,1,0:T(8,128)S(1)}, f32[3,1,16,256]{3,2,1,0:T(8,128)S(1)}, u32[]{:S(2)}, u32[]{:S(2)}) collective-permute-start(f32[3,1,16,256]{3,2,1,0:T(8,128)S(1)} %get-tuple-element.15), channel_id=1, source_target_pairs={{0,16},{1,17},{2,18},{3,19},{4,20},{5,21},{6,22},{7,23},{8,24},{9,... | collective-permute-start | bytes 147464 | tf_op jit(solution)/shard_map/ppermute | solution.py:20
  94.8 28.6 %collective-permute-start.14 = (f32[3,18,1,256]{3,2,1,0:T(1,128)S(1)}, f32[3,18,1,256]{3,2,1,0:T(1,128)S(1)}, u32[]{:S(2)}, u32[]{:S(2)}) collective-permute-start(f32[3,18,1,256]{3,2,1,0:T(1,128)S(1)} %get-tuple-element.31), channel_id=1, source_target_pairs={{4,0},{8,4},{12,8},{5,1},{9,5},{13,9},{6,2},{10,6},{14,10},{7,3},{... | collective-permute-start | bytes 165896 | tf_op jit(solution)/shard_map/ppermute | solution.py:23
  96.1 27.3 %collective-permute-start.15 = (f32[3,18,1,256]{3,2,1,0:T(1,128)S(1)}, f32[3,18,1,256]{3,2,1,0:T(1,128)S(1)}, u32[]{:S(2)}, u32[]{:S(2)}) collective-permute-start(f32[3,18,1,256]{3,2,1,0:T(1,128)S(1)} %get-tuple-element.32), channel_id=1, source_target_pairs={{0,4},{4,8},{8,12},{1,5},{5,9},{9,13},{2,6},{6,10},{10,14},{3,7},{... | collective-permute-start | bytes 165896 | tf_op jit(solution)/shard_map/ppermute | solution.py:20
  102.3 12.5 %collective-permute-start.16 = (f32[3,16,16,1]{3,2,1,0:T(8,128)S(1)}, f32[3,16,16,1]{3,2,1,0:T(8,128)S(1)}, u32[]{:S(2)}, u32[]{:S(2)}) collective-permute-start(f32[3,16,16,1]{3,2,1,0:T(8,128)S(1)} %get-tuple-element.17), channel_id=1, source_target_pairs={{1,0},{2,1},{3,2},{0,3},{5,4},{6,5},{7,6},{4,7},{9,8},{10,9},{11,1... | collective-permute-start | bytes 9224 | tf_op jit(solution)/shard_map/ppermute | solution.py:23
  106.0 17.3 %collective-permute-start.17 = (f32[3,16,16,1]{3,2,1,0:T(8,128)S(1)}, f32[3,16,16,1]{3,2,1,0:T(8,128)S(1)}, u32[]{:S(2)}, u32[]{:S(2)}) collective-permute-start(f32[3,16,16,1]{3,2,1,0:T(8,128)S(1)} %get-tuple-element.18), channel_id=1, source_target_pairs={{0,1},{1,2},{2,3},{3,0},{4,5},{5,6},{6,7},{7,4},{8,9},{9,10},{10,1... | collective-permute-start | bytes 9224 | tf_op jit(solution)/shard_map/ppermute | solution.py:20
  124.2 1.1 copy-start.2
  158.3 0.9 copy-start.3
where the time goes:
time: 160 us; the launch traced here: 159 us
  waiting for transfers between devices  50 us (31%)
  starting transfers between devices  43.1 us (27%)
  blocking collectives  30.4 us (19%)
  other arithmetic  17.4 us (11%)
  local copies, waits for them, and re-layouts  16.6 us (10%)
  between operations  1.73 us (1%)
    ppermute x9, starting transfers between devices, with_halo(): lax.ppermute(lax.slice_in_dim(block, block.shape[dim] - width, None, axis...  25.7 us
    ppermute x9, waiting for transfers between devices, with_halo(): lax.ppermute(lax.slice_in_dim(block, block.shape[dim] - width, None, axis...  25.2 us
    ppermute x9, waiting for transfers between devices, with_halo(): lax.ppermute(lax.slice_in_dim(block, 0, width, axis=dim), axis, backward)  24.8 us
    psum x1, blocking collectives, per_device(): line_num, line_den = lax.psum((num_part, den_part), 'gz')  18 us
    ppermute x9, starting transfers between devices, with_halo(): lax.ppermute(lax.slice_in_dim(block, 0, width, axis=dim), axis, backward)  17.4 us
    pmax x1, blocking collectives, per_device(): peak_coef = lax.pmax(jnp.max(line_coef), ('gx', 'gy'))  12.4 us
    add x3, other arithmetic, box_three(): return 0.25 * lower_side + 0.5 * middle + 0.25 * upper_side  9.64 us
    unnamed x16, local copies, waits for them, and re-layouts  6.82 us
  transfers between devices with their start and end apart: 18, of which 12 were waited for; matrix products, arithmetic and copies ran while one was open for 4% of the time, Pallas kernels for 0%

commit v1 on v0

v1 whole, which is shorter than its diff:
```python
import functools

import jax
import jax.numpy as jnp
from jax import lax
from jax.experimental import pallas as pl
from jax.experimental.pallas import tpu as pltpu
from jax.sharding import PartitionSpec as P

MESH = pl.DeviceIdType.MESH
pairs = ((0, 0), (1, 1), (2, 2), (0, 1), (0, 2), (1, 2))
pair_weight = (1.0, 1.0, 1.0, 2.0, 2.0, 2.0)
eps_line = 1e-06
offsets = [(dx, dy, dz) for dz in (1, -1, 0) for dx in (0, 1, -1) for dy in (0, 1, -1) if (dx, dy, dz) != (0, 0, 0)]


def edge_slots(nx):
    ends = [0, 1, nx - 2, nx - 1]
    order = [(f, x) for f in range(6) for x in ends] + [(f, x) for f in range(6) for x in range(2, nx - 2)]
    return {key: 2 * n for n, key in enumerate(order)}


def kernel(sizes, vel, met, visc, coef_out, V, Gv, G, H, D, Q, PK, R, LS, PS, sem_in, send, recv, lsend, lrecv, psend, precv):
    NX, NY, NZ = sizes
    nx, ny, nz = vel.shape[1:]
    yr, zr = ny + 8, nz + 128
    slots = edge_slots(nx)
    lanes_packed = PK.shape[2]
    ix, iy, iz = lax.axis_index("gx"), lax.axis_index("gy"), lax.axis_index("gz")

    load_v = pltpu.make_async_copy(vel, V.at[0:3, 2 : 2 + nx, 0:ny, 0:nz], sem_in.at[0])
    load_m = pltpu.make_async_copy(met, V.at[3:6, 2 : 2 + nx, 0:ny, 0:nz], sem_in.at[1])
    load_v.start()
    load_m.start()

    def exists(d):
        ok = None
        for delta, i, n in ((d[0], ix, NX), (d[1], iy, NY)):
            if delta:
                c = (i + delta >= 0) & (i + delta < n)
                ok = c if ok is None else ok & c
        return ok

    def when(cond, fn):
        if cond is None:
            fn()
        else:
            pl.when(cond)(fn)

    def dev(d):
        return (ix + d[0], iy + d[1], lax.rem(iz + d[2] + NZ, NZ))

    zplane = jnp.zeros((yr, zr), jnp.float32)
    for f in range(6):
        for xi in (0, 1, nx + 2, nx + 3):
            V[f, xi] = zplane
        def clear(x, _, f=f):
            V[f, x, ny:yr, :] = zplane[0:8]
            return 0
        lax.fori_loop(2, 2 + nx, clear, 0)
    for s in range(2):
        for dx in range(3):
            for dy in range(3):
                R[s, dx, dy] = jnp.zeros((ny, lanes_packed), jnp.float32)

    barrier = pltpu.get_barrier_semaphore()
    expected = jnp.int32(0)
    for d in offsets:
        ok = exists(d)
        def sig(d=d):
            pl.semaphore_signal(barrier, inc=1, device_id=dev(d), device_id_type=MESH)
        when(ok, sig)
        expected = expected + (1 if ok is None else ok.astype(jnp.int32))
    for o in range(1, NZ):
        pl.semaphore_signal(barrier, inc=1, device_id=(ix, iy, lax.rem(iz + o, NZ)), device_id_type=MESH)
    plane_peers = [(a, b) for a in range(NX) for b in range(NY) if (a, b) != (0, 0)]
    for a, b in plane_peers:
        pl.semaphore_signal(barrier, inc=1, device_id=(lax.rem(ix + a, NX), lax.rem(iy + b, NY), iz), device_id_type=MESH)
    expected = expected + (NZ - 1 + len(plane_peers))

    load_v.wait()
    load_m.wait()

    lane = lax.broadcasted_iota(jnp.int32, (ny, 128), 1)
    half = lane // 2
    acc = [[jnp.zeros((ny, 128), jnp.float32) for _ in range(lanes_packed // 128)] for _ in range(2)]
    for (f, x), p in slots.items():
        t, l = divmod(p, 128)
        here = half == l // 2
        hi = V[f, x + 2, 0:ny, nz - 128 : nz]
        lo = V[f, x + 2, 0:ny, 0:128]
        s_hi, s_lo = (l - 126) % 128, l
        acc[0][t] = jnp.where(here, pltpu.roll(hi, s_hi, 1) if s_hi else hi, acc[0][t])
        acc[1][t] = jnp.where(here, pltpu.roll(lo, s_lo, 1) if s_lo else lo, acc[1][t])
    for s in range(2):
        for t in range(lanes_packed // 128):
            PK[s, :, 128 * t : 128 * t + 128] = acc[s][t]

    pl.semaphore_wait(barrier, expected)

    def span_x(dx, metric):
        if dx == 0:
            return (2, 2, nx)
        if dx == 1:
            return (nx + 1, 1, 1) if metric else (nx, 0, 2)
        return (2, nx + 2, 1) if metric else (2, nx + 2, 2)

    def span_y(dy, metric):
        if dy == 0:
            return (0, 0, ny)
        if dy == 1:
            return (ny - 1, ny + 7, 1) if metric else (ny - 2, ny + 6, 2)
        return (0, ny, 1) if metric else (0, ny, 2)

    def copies(n, d):
        dx, dy, dz = d
        out = []
        if dz:
            s = 0 if dz == 1 else 1
            r0, rn = (0, ny) if dy == 0 else ((ny - 8, 8) if dy == 1 else (0, 8))
            ln = lanes_packed if dx == 0 else 128
            out.append((PK.at[s, r0 : r0 + rn, 0:ln], R.at[s, dx + 1, dy + 1, r0 : r0 + rn, 0:ln], 2 * n))
        else:
            for k in range(2):
                xs, xd, xn = span_x(dx, k == 1)
                ys, yd, yn = span_y(dy, k == 1)
                f0 = 3 * k
                out.append((
                    V.at[f0 : f0 + 3, xs : xs + xn, ys : ys + yn, 0:nz],
                    V.at[f0 : f0 + 3, xd : xd + xn, yd : yd + yn, 0:nz],
                    2 * n + k,
                ))
        return [
            pltpu.make_async_remote_copy(src_ref=a, dst_ref=b, send_sem=send.at[j], recv_sem=recv.at[j], device_id=dev(d), device_id_type=MESH)
            for a, b, j in out
        ]

    for n, d in enumerate(offsets):
        def go(n=n, d=d):
            for c in copies(n, d):
                c.start()
        when(exists(d), go)
    for n, d in enumerate(offsets):
        def land(n=n, d=d):
            for c in copies(n, d):
                c.wait_recv()
        when(exists((-d[0], -d[1], -d[2])), land)
    for n, d in enumerate(offsets):
        def left(n=n, d=d):
            for c in copies(n, d):
                c.wait_send()
        when(exists(d), left)

    lane_r = lax.broadcasted_iota(jnp.int32, (yr, 128), 1)
    low_rows = lax.broadcasted_iota(jnp.int32, (8, 128), 0) < 4
    def packed(s, dx, t):
        cut = slice(128 * t, 128 * t + 128)
        edge = jnp.where(low_rows, R[s, dx, 0, 0:8, cut], R[s, dx, 2, ny - 8 : ny, cut])
        return jnp.concatenate([R[s, dx, 1, :, cut], edge], axis=0)
    tiles = {}
    for f in range(6):
        for xi in range(nx + 4):
            if f >= 3 and xi in (0, nx + 3):
                continue
            if xi < 2:
                dx, x = 2, nx - 2 + xi
            elif xi >= nx + 2:
                dx, x = 0, xi - nx - 2
            else:
                dx, x = 1, xi - 2
            t, l = divmod(slots[(f, x)], 128)
            for s in range(2):
                if (s, dx, t) not in tiles:
                    tiles[(s, dx, t)] = packed(s, dx, t)
            a = pltpu.roll(tiles[(0, dx, t)], (126 - l) % 128, 1) if l != 126 else tiles[(0, dx, t)]
            b = pltpu.roll(tiles[(1, dx, t)], (128 - l) % 128, 1) if l else tiles[(1, dx, t)]
            V[f, xi, :, nz:zr] = jnp.where(lane_r < 64, b, a)

    def up(a, axis):
        return pltpu.roll(a, a.shape[axis] - 1, axis)

    def down(a, axis):
        return pltpu.roll(a, 1, axis)

    def smooth(a, axis):
        t = a + down(a, axis)
        return t + up(t, axis)

    def velocity_plane(x, _):
        for c in range(3):
            Gv[c, x] = smooth(smooth(V[c, x], 0), 1)
        return 0

    lax.fori_loop(0, nx + 4, velocity_plane, 0)

    def strains(load, m, x):
        d = [[None] * 3 for _ in range(3)]
        for i in range(3):
            here = load(i, x)
            d[i][0] = m[0] * (load(i, x + 1) - load(i, x - 1))
            d[i][1] = m[1] * (up(here, 0) - down(here, 0))
            d[i][2] = m[2] * (up(here, 1) - down(here, 1))
        e = [d[a][b] if a == b else 0.5 * (d[a][b] + d[b][a]) for a, b in pairs]
        square = (e[0] * e[0] + e[1] * e[1] + e[2] * e[2]) + 2.0 * (e[3] * e[3] + e[4] * e[4] + e[5] * e[5])
        return e, jnp.sqrt(0.5 * square)

    def field_plane(x, _):
        m = [V[3 + c, x] for c in range(3)]
        e, mag = strains(lambda i, p: V[i, p], m, x)
        p = m[0][0:ny, 0:nz] * m[1][0:ny, 0:nz] * m[2][0:ny, 0:nz]
        dq = jnp.exp((-2.0 / 3.0) * jnp.log(p))
        Q[x] = dq
        D[x] = dq * mag[0:ny, 0:nz]
        for k, (a, b) in enumerate(pairs):
            G[k, x] = smooth(smooth(V[a, x] * V[b, x], 0)[0:ny], 1)[:, 0:nz]
            G[6 + k, x] = smooth(smooth(mag * e[k], 0)[0:ny], 1)[:, 0:nz]
        return 0

    lax.fori_loop(1, nx + 3, field_plane, 0)

    row = lax.broadcasted_iota(jnp.int32, (yr, zr), 0)
    has_lo = jnp.where(iy > 0, 1.0, 0.0)
    has_hi = jnp.where(iy < NY - 1, 1.0, 0.0)
    row_scale = jnp.where(row < ny, 1.0, jnp.where(row == ny, has_hi, has_lo)) * (1.0 / 64.0)

    def hat_plane(x, _):
        inside = jnp.where((x == 1) & (ix == 0), 0.0, jnp.where((x == nx + 2) & (ix == NX - 1), 0.0, 1.0))
        for c in range(3):
            mid = Gv[c, x]
            H[c, x] = (Gv[c, x - 1] + Gv[c, x + 1] + (mid + mid)) * (row_scale * inside)
        return 0

    lax.fori_loop(1, nx + 3, hat_plane, 0)

    lane_s = lax.broadcasted_iota(jnp.int32, (ny, 128), 1)

    def line_plane(x, sums):
        d = [[None] * 3 for _ in range(3)]
        hat = []
        for i in range(3):
            here = H[i, x]
            core = here[0:ny]
            hat.append(core[:, 0:nz])
            d[i][0] = V[3, x, 0:ny, 0:nz] * (H[i, x + 1, 0:ny, 0:nz] - H[i, x - 1, 0:ny, 0:nz])
            d[i][1] = V[4, x, 0:ny, 0:nz] * (up(here, 0) - down(here, 0))[0:ny, 0:nz]
            d[i][2] = V[5, x, 0:ny, 0:nz] * (up(core, 1) - down(core, 1))[:, 0:nz]
        e = [d[a][b] if a == b else 0.5 * (d[a][b] + d[b][a]) for a, b in pairs]
        square = (e[0] * e[0] + e[1] * e[1] + e[2] * e[2]) + 2.0 * (e[3] * e[3] + e[4] * e[4] + e[5] * e[5])
        mag2 = 2.0 * jnp.sqrt(0.5 * square)
        num = den = 0.0
        for k, (a, b) in enumerate(pairs):
            vv, ms = G[k, x], G[6 + k, x]
            vv = (G[k, x - 1] + G[k, x + 1] + (vv + vv)) * (1.0 / 64.0)
            ms = (G[6 + k, x - 1] + G[6 + k, x + 1] + (ms + ms)) * (1.0 / 128.0)
            leonard = vv - hat[a] * hat[b]
            model = ms - mag2 * e[k]
            n, m2 = leonard * model, model * model
            if pair_weight[k] != 1.0:
                n, m2 = pair_weight[k] * n, pair_weight[k] * m2
            num, den = num + n, den + m2
        dq2 = 2.0 * Q[x]
        num = num * dq2
        den = den * (dq2 * dq2)
        num = jnp.sum(num, axis=1, keepdims=True)
        den = jnp.sum(den, axis=1, keepdims=True)
        sums = jnp.where(lane_s == x - 2, num, sums)
        return jnp.where(lane_s == x + 62, den, sums)

    sums = lax.fori_loop(2, nx + 2, line_plane, jnp.zeros((ny, 128), jnp.float32))

    LS[iz] = sums
    def line_copy(o):
        return pltpu.make_async_remote_copy(
            src_ref=LS.at[iz], dst_ref=LS.at[iz], send_sem=lsend.at[o - 1], recv_sem=lrecv.at[o - 1],
            device_id=(ix, iy, lax.rem(iz + o, NZ)), device_id_type=MESH)
    def line_landing(o):
        src = lax.rem(iz - o + NZ, NZ)
        return pltpu.make_async_remote_copy(
            src_ref=LS.at[src], dst_ref=LS.at[src], send_sem=lsend.at[o - 1], recv_sem=lrecv.at[o - 1],
            device_id=(ix, iy, lax.rem(iz + o, NZ)), device_id_type=MESH)
    for o in range(1, NZ):
        line_copy(o).start()
    for o in range(1, NZ):
        line_landing(o).wait_recv()
    total = LS[0]
    for o in range(1, NZ):
        total = total + LS[o]
    cells = float(nz * NZ)
    line_num = total / cells
    line_den = pltpu.roll(total, 64, 1) / cells
    coef = line_num / (line_den + eps_line)
    here_max = jnp.max(jnp.where(lane_s < nx, coef, -jnp.inf), axis=(0, 1), keepdims=True)
    me = ix * NY + iy
    PS[me] = jnp.broadcast_to(here_max, (8, 128))
    def peak_copy(j, a, b, landing):
        tx, ty = lax.rem(ix + a, NX), lax.rem(iy + b, NY)
        slot = me
        if landing:
            slot = lax.rem(ix - a + NX, NX) * NY + lax.rem(iy - b + NY, NY)
        return pltpu.make_async_remote_copy(
            src_ref=PS.at[slot], dst_ref=PS.at[slot], send_sem=psend.at[j], recv_sem=precv.at[j],
            device_id=(tx, ty, iz), device_id_type=MESH)
    for j, (a, b) in enumerate(plane_peers):
        peak_copy(j, a, b, False).start()
    for o in range(1, NZ):
        line_copy(o).wait_send()
    for j, (a, b) in enumerate(plane_peers):
        peak_copy(j, a, b, True).wait_recv()
    peak = PS[0]
    for j in range(1, NX * NY):
        peak = jnp.maximum(peak, PS[j])
    coef = jnp.minimum(coef, 0.5 * peak[0:1, :])
    for x in range(nx):
        column = jnp.sum(jnp.where(lane_s == x, coef, 0.0), axis=1, keepdims=True)
        visc[x] = D[x + 2] * column
    coef_out[...] = coef
    for j, (a, b) in enumerate(plane_peers):
        peak_copy(j, a, b, False).wait_send()


def per_device(sizes, velocity, metric):
    nx, ny, nz = velocity.shape[1:]
    NX, NY, NZ = sizes
    yr, zr = ny + 8, nz + 128
    packed = -(-12 * nx // 128) * 128
    f32 = jnp.float32
    visc, coef = pl.pallas_call(
        functools.partial(kernel, sizes),
        out_shape=(jax.ShapeDtypeStruct((nx, ny, nz), f32), jax.ShapeDtypeStruct((ny, 128), f32)),
        in_specs=[pl.BlockSpec(memory_space=pl.ANY)] * 2,
        out_specs=(pl.BlockSpec(memory_space=pltpu.VMEM),) * 2,
        scratch_shapes=[
            pltpu.VMEM((6, nx + 4, yr, zr), f32),
            pltpu.VMEM((3, nx + 4, yr, zr), f32),
            pltpu.VMEM((12, nx + 4, ny, nz), f32),
            pltpu.VMEM((3, nx + 4, yr, zr), f32),
            pltpu.VMEM((nx + 4, ny, nz), f32),
            pltpu.VMEM((nx + 4, ny, nz), f32),
            pltpu.VMEM((2, ny, packed), f32),
            pltpu.VMEM((2, 3, 3, ny, packed), f32),
            pltpu.VMEM((NZ, ny, 128), f32),
            pltpu.VMEM((NX * NY, 8, 128), f32),
            pltpu.SemaphoreType.DMA((2,)),
            pltpu.SemaphoreType.DMA((2 * len(offsets),)),
            pltpu.SemaphoreType.DMA((2 * len(offsets),)),
            pltpu.SemaphoreType.DMA((NZ,)),
            pltpu.SemaphoreType.DMA((NZ,)),
            pltpu.SemaphoreType.DMA((NX * NY,)),
            pltpu.SemaphoreType.DMA((NX * NY,)),
        ],
        compiler_params=pltpu.CompilerParams(collective_id=0, has_side_effects=True, vmem_limit_bytes=48 * 1024 * 1024),
    )(velocity, metric)
    return visc, coef[:, :nx].T


def solution(mesh):
    sizes = (mesh.shape["gx"], mesh.shape["gy"], mesh.shape["gz"])
    return jax.shard_map(
        functools.partial(per_device, sizes),
        mesh=mesh,
        in_specs=(P(None, "gx", "gy", "gz"), P(None, "gx", "gy", "gz")),
        out_specs=(P("gx", "gy", "gz"), P("gx", "gy")),
        check_vma=False,
    )
```

time: 160 us -> 42.7 us (0.27)
  waiting for transfers between devices: 50 us -> 0 us
  starting transfers between devices: 43.1 us -> 0 us
  Pallas kernels: 0 us -> 38.2 us
  blocking collectives: 30.4 us -> 0 us
  other arithmetic: 17.4 us -> 0 us
  local copies, waits for them, and re-layouts: 16.6 us -> 3.63 us
    ppermute x18 -> x0, waiting for transfers between devices: 50 us -> none  [the longest x9 25.2 us: with_halo(): lax.ppermute(lax.slice_in_dim(block, block.shape[dim] - width, None, axis...]
    ppermute x18 -> x0, starting transfers between devices: 43.1 us -> none  [the longest x9 25.7 us: with_halo(): lax.ppermute(lax.slice_in_dim(block, block.shape[dim] - width, None, axis...]
    pallas_call x0 -> x1, Pallas kernels: none -> 38.2 us  [per_device(): pl.pallas_call(functools.partial(kernel, sizes), out_shape=(jax.ShapeDtyp...]
    psum x1 -> x0, blocking collectives: 18 us -> none  [per_device(): line_num, line_den = lax.psum((num_part, den_part), 'gz')]
    pmax x1 -> x0, blocking collectives: 12.4 us -> none  [per_device(): peak_coef = lax.pmax(jnp.max(line_coef), ('gx', 'gy'))]
    add x3 -> x0, other arithmetic: 9.64 us -> none  [box_three(): return 0.25 * lower_side + 0.5 * middle + 0.25 * upper_side]
    slice x11 -> x0, local copies, waits for them, and re-layouts: 5.06 us -> none  [the longest x5 2.56 us: with_halo(): lax.slice_in_dim(block, block.shape[dim] - width, None, axis=dim)]
    ppermute x4 -> x0, local copies, waits for them, and re-layouts: 4.73 us -> none  [the longest x2 3.01 us: with_halo(): lax.ppermute(lax.slice_in_dim(block, 0, width, axis=dim), axis, backward)]
  transfers between devices with their start and end apart: 18 -> 0, of which waited for: 12 -> 0; matrix products, arithmetic and copies ran while one was open for 4% -> 0% of each run, Pallas kernels for 0% -> 0%
where the time goes in v1:
time: 42.7 us; the launch traced here: 42.5 us
  Pallas kernels  38.2 us (89%)
  local copies, waits for them, and re-layouts  3.63 us (9%)
  between operations  0.66 us (2%)
    pallas_call x1, Pallas kernels, per_device(): pl.pallas_call(functools.partial(kernel, sizes), out_shape=(jax.ShapeDtyp...  38.2 us
    unnamed x6, local copies, waits for them, and re-layouts  3.63 us

profile of v1, /device:TPU:0, one launch (start us, length us, event | category | flops | bytes accessed | tf_op | source)
XLA Modules:
  0.0 42.5 jit_solution(15333409403520077288)
XLA Ops:
  0.6 0.0 copy-start
  0.6 1.1 %copy-done = f32[3,16,16,256]{3,2,1,0:T(8,128)S(1)} copy-done((f32[3,16,16,256]{3,2,1,0:T(8,128)S(1)}, f32[3,16,16,256]{3,2,1,0:T(8,128)}, u32[]{:S(2)}) %copy-start) | copy-done | bytes 786456
  1.8 0.0 copy-start.1
  1.8 1.1 %copy-done.1 = f32[3,16,16,256]{3,2,1,0:T(8,128)S(1)} copy-done((f32[3,16,16,256]{3,2,1,0:T(8,128)S(1)}, f32[3,16,16,256]{3,2,1,0:T(8,128)}, u32[]{:S(2)}) %copy-start.1) | copy-done | bytes 786456
  2.9 38.2 %shard_map.41 = (f32[16,16,256]{2,1,0:T(8,128)S(1)}, f32[16,128]{1,0:T(8,128)S(1)}) custom-call(f32[3,16,16,256]{3,2,1,0:T(8,128)S(1)} %copy-done, f32[3,16,16,256]{3,2,1,0:T(8,128)S(1)} %copy-done.1), custom_call_target="tpu_custom_call" | custom-call | tf_op jit(solution)/shard_map/pallas_call | solution.py:327
  41.1 0.7 %copy.4 = f32[16,16]{1,0:T(8,128)} copy(f32[16,16]{0,1:T(8,128)S(1)} %slice_bitcast_fusion) | data formatting | bytes 2048
  41.8 0.7 %copy.6 = f32[16,16,256]{2,1,0:T(8,128)} copy(f32[16,16,256]{2,1,0:T(8,128)S(1)} %get-tuple-element.10) | data formatting | bytes 524288
  (1 shorter events, 0.0 us)
Async XLA Ops:
  0.6 1.1 %copy-start = (f32[3,16,16,256]{3,2,1,0:T(8,128)S(1)}, f32[3,16,16,256]{3,2,1,0:T(8,128)}, u32[]{:S(2)}) copy-start(f32[3,16,16,256]{3,2,1,0:T(8,128)} %vel.1) | copy-start | bytes 2359300
  1.8 1.1 %copy-start.1 = (f32[3,16,16,256]{3,2,1,0:T(8,128)S(1)}, f32[3,16,16,256]{3,2,1,0:T(8,128)}, u32[]{:S(2)}) copy-start(f32[3,16,16,256]{3,2,1,0:T(8,128)} %met.1) | copy-start | bytes 2359300

commit v2 on v1

--- a/solution.py
+++ b/solution.py
@@ -20,7 +20,7 @@
     return {key: 2 * n for n, key in enumerate(order)}
 
 
-def kernel(sizes, vel, met, visc, coef_out, V, Gv, G, H, D, Q, PK, R, LS, PS, sem_in, send, recv, lsend, lrecv, psend, precv):
+def kernel(sizes, vel, met, D, coef_out, V, Gv, G, H, Q, PK, R, LS, PS, sem_in, send, recv, lsend, lrecv, psend, precv):
     NX, NY, NZ = sizes
     nx, ny, nz = vel.shape[1:]
     yr, zr = ny + 8, nz + 128
@@ -140,16 +140,15 @@
             for c in copies(n, d):
                 c.start()
         when(exists(d), go)
-    for n, d in enumerate(offsets):
-        def land(n=n, d=d):
-            for c in copies(n, d):
-                c.wait_recv()
-        when(exists((-d[0], -d[1], -d[2])), land)
-    for n, d in enumerate(offsets):
-        def left(n=n, d=d):
-            for c in copies(n, d):
-                c.wait_send()
-        when(exists(d), left)
+    def land(wanted):
+        for n, d in enumerate(offsets):
+            if wanted(d):
+                def arrive(n=n, d=d):
+                    for c in copies(n, d):
+                        c.wait_recv()
+                when(exists((-d[0], -d[1], -d[2])), arrive)
+
+    land(lambda d: d[0] == 0 and d[2] != 0)
 
     lane_r = lax.broadcasted_iota(jnp.int32, (yr, 128), 1)
     low_rows = lax.broadcasted_iota(jnp.int32, (8, 128), 0) < 4
@@ -158,8 +157,8 @@
         edge = jnp.where(low_rows, R[s, dx, 0, 0:8, cut], R[s, dx, 2, ny - 8 : ny, cut])
         return jnp.concatenate([R[s, dx, 1, :, cut], edge], axis=0)
     tiles = {}
-    for f in range(6):
-        for xi in range(nx + 4):
+    def fill_span(f, planes):
+        for xi in planes:
             if f >= 3 and xi in (0, nx + 3):
                 continue
             if xi < 2:
@@ -176,6 +175,10 @@
             b = pltpu.roll(tiles[(1, dx, t)], (128 - l) % 128, 1) if l else tiles[(1, dx, t)]
             V[f, xi, :, nz:zr] = jnp.where(lane_r < 64, b, a)
 
+    for f in range(6):
+        fill_span(f, range(2, nx + 2))
+    land(lambda d: d[0] == 0 and d[2] == 0)
+
     def up(a, axis):
         return pltpu.roll(a, a.shape[axis] - 1, axis)
 
@@ -183,6 +186,8 @@
         return pltpu.roll(a, 1, axis)
 
     def smooth(a, axis):
+        if axis == 1:
+            return (a + a) + (up(a, 1) + down(a, 1))
         t = a + down(a, axis)
         return t + up(t, axis)
 
@@ -191,7 +196,6 @@
             Gv[c, x] = smooth(smooth(V[c, x], 0), 1)
         return 0
 
-    lax.fori_loop(0, nx + 4, velocity_plane, 0)
 
     def strains(load, m, x):
         d = [[None] * 3 for _ in range(3)]
@@ -210,13 +214,19 @@
         p = m[0][0:ny, 0:nz] * m[1][0:ny, 0:nz] * m[2][0:ny, 0:nz]
         dq = jnp.exp((-2.0 / 3.0) * jnp.log(p))
         Q[x] = dq
-        D[x] = dq * mag[0:ny, 0:nz]
+        D[jnp.clip(x - 2, 0, nx - 1)] = dq * mag[0:ny, 0:nz]
         for k, (a, b) in enumerate(pairs):
             G[k, x] = smooth(smooth(V[a, x] * V[b, x], 0)[0:ny], 1)[:, 0:nz]
             G[6 + k, x] = smooth(smooth(mag * e[k], 0)[0:ny], 1)[:, 0:nz]
         return 0
 
-    lax.fori_loop(1, nx + 3, field_plane, 0)
+    lax.fori_loop(2, nx + 2, velocity_plane, 0, unroll=4)
+    lax.fori_loop(3, nx + 1, field_plane, 0)
+    land(lambda d: d[0] != 0)
+    for f in range(6):
+        fill_span(f, (0, 1, nx + 2, nx + 3))
+    lax.fori_loop(0, 4, lambda i, c: velocity_plane(jnp.where(i < 2, i, nx + i), c), 0)
+    lax.fori_loop(0, 4, lambda i, c: field_plane(jnp.where(i < 2, i + 1, nx + 4 - i), c), 0)
 
     row = lax.broadcasted_iota(jnp.int32, (yr, zr), 0)
     has_lo = jnp.where(iy > 0, 1.0, 0.0)
@@ -266,7 +276,7 @@
         sums = jnp.where(lane_s == x - 2, num, sums)
         return jnp.where(lane_s == x + 62, den, sums)
 
-    sums = lax.fori_loop(2, nx + 2, line_plane, jnp.zeros((ny, 128), jnp.float32))
+    sums = lax.fori_loop(2, nx + 2, line_plane, jnp.zeros((ny, 128), jnp.float32), unroll=2)
 
     LS[iz] = sums
     def line_copy(o):
@@ -289,9 +299,12 @@
     line_num = total / cells
     line_den = pltpu.roll(total, 64, 1) / cells
     coef = line_num / (line_den + eps_line)
-    here_max = jnp.max(jnp.where(lane_s < nx, coef, -jnp.inf), axis=(0, 1), keepdims=True)
+    masked = jnp.where(lane_s < nx, coef, -jnp.inf)
+    here_max = masked[0:8]
+    for r in range(8, ny, 8):
+        here_max = jnp.maximum(here_max, masked[r : r + 8])
     me = ix * NY + iy
-    PS[me] = jnp.broadcast_to(here_max, (8, 128))
+    PS[me] = here_max
     def peak_copy(j, a, b, landing):
         tx, ty = lax.rem(ix + a, NX), lax.rem(iy + b, NY)
         slot = me
@@ -309,13 +322,25 @@
     peak = PS[0]
     for j in range(1, NX * NY):
         peak = jnp.maximum(peak, PS[j])
-    coef = jnp.minimum(coef, 0.5 * peak[0:1, :])
-    for x in range(nx):
-        column = jnp.sum(jnp.where(lane_s == x, coef, 0.0), axis=1, keepdims=True)
-        visc[x] = D[x + 2] * column
+    coef = jnp.minimum(coef, 0.5 * jnp.max(peak, axis=(0, 1), keepdims=True))
     coef_out[...] = coef
     for j, (a, b) in enumerate(plane_peers):
         peak_copy(j, a, b, False).wait_send()
+    for n, d in enumerate(offsets):
+        def left(n=n, d=d):
+            for c in copies(n, d):
+                c.wait_send()
+        when(exists(d), left)
+
+
+def scale_kernel(D, coef, visc, coef_out):
+    nx, ny = visc.shape[:2]
+    lane = lax.broadcasted_iota(jnp.int32, (ny, 128), 1)
+    table = coef[...]
+    for x in range(nx):
+        column = jnp.sum(jnp.where(lane == x, table, 0.0), axis=1, keepdims=True)
+        visc[x] = D[x] * column
+    coef_out[...] = table.T[0:nx, :]
 
 
 def per_device(sizes, velocity, metric):
@@ -324,17 +349,16 @@
     yr, zr = ny + 8, nz + 128
     packed = -(-12 * nx // 128) * 128
     f32 = jnp.float32
-    visc, coef = pl.pallas_call(
+    dmag, coef = pl.pallas_call(
         functools.partial(kernel, sizes),
         out_shape=(jax.ShapeDtypeStruct((nx, ny, nz), f32), jax.ShapeDtypeStruct((ny, 128), f32)),
-        in_specs=[pl.BlockSpec(memory_space=pl.ANY)] * 2,
+        in_specs=[pl.BlockSpec(memory_space=pltpu.HBM)] * 2,
         out_specs=(pl.BlockSpec(memory_space=pltpu.VMEM),) * 2,
         scratch_shapes=[
             pltpu.VMEM((6, nx + 4, yr, zr), f32),
             pltpu.VMEM((3, nx + 4, yr, zr), f32),
             pltpu.VMEM((12, nx + 4, ny, nz), f32),
             pltpu.VMEM((3, nx + 4, yr, zr), f32),
-            pltpu.VMEM((nx + 4, ny, nz), f32),
             pltpu.VMEM((nx + 4, ny, nz), f32),
             pltpu.VMEM((2, ny, packed), f32),
             pltpu.VMEM((2, 3, 3, ny, packed), f32),
@@ -348,9 +372,15 @@
             pltpu.SemaphoreType.DMA((NX * NY,)),
             pltpu.SemaphoreType.DMA((NX * NY,)),
         ],
-        compiler_params=pltpu.CompilerParams(collective_id=0, has_side_effects=True, vmem_limit_bytes=48 * 1024 * 1024),
+        compiler_params=pltpu.CompilerParams(collective_id=0, has_side_effects=True, vmem_limit_bytes=67043328 - 600 * 1024),
     )(velocity, metric)
-    return visc, coef[:, :nx].T
+    return pl.pallas_call(
+        scale_kernel,
+        out_shape=(jax.ShapeDtypeStruct((nx, ny, nz), f32), jax.ShapeDtypeStruct((nx, ny), f32)),
+        in_specs=[pl.BlockSpec(memory_space=pltpu.VMEM)] * 2,
+        out_specs=(pl.BlockSpec(memory_space=pltpu.VMEM),) * 2,
+        compiler_params=pltpu.CompilerParams(vmem_limit_bytes=4 * 1024 * 1024),
+    )(dmag, coef)
 
 
 def solution(mesh):

time: 42.7 us -> 35.9 us (0.84)
  Pallas kernels: 38.2 us -> 33.4 us
  local copies, waits for them, and re-layouts: 3.63 us -> 1.64 us
    pallas_call x1, Pallas kernels: 38.2 us -> 32.6 us  [per_device(): pl.pallas_call(functools.partial(kernel, sizes), out_shape=(jax.ShapeDtyp...]
    unnamed x6 -> x4, local copies, waits for them, and re-layouts: 3.63 us -> 1.64 us
    pallas_call x0 -> x1, Pallas kernels: none -> 0.81 us  [per_device(): pl.pallas_call(scale_kernel, out_shape=(jax.ShapeDtypeStruct((nx, ny, nz)...]
where the time goes in v2:
time: 35.9 us; the launch traced here: 35.7 us
  Pallas kernels  33.4 us (93%)
  local copies, waits for them, and re-layouts  1.64 us (5%)
  between operations  0.65 us (2%)
    pallas_call x1, Pallas kernels, per_device(): pl.pallas_call(functools.partial(kernel, sizes), out_shape=(jax.ShapeDtyp...  32.6 us
    unnamed x4, local copies, waits for them, and re-layouts  1.64 us
    pallas_call x1, Pallas kernels, per_device(): pl.pallas_call(scale_kernel, out_shape=(jax.ShapeDtypeStruct((nx, ny, nz)...  0.81 us

profile of v2, /device:TPU:0, one launch (start us, length us, event | category | flops | bytes accessed | tf_op | source)
XLA Modules:
  0.0 35.7 jit_solution(4824935381344407135)
XLA Ops:
  0.6 32.6 %shard_map.41 = (f32[16,16,256]{2,1,0:T(8,128)}, f32[16,128]{1,0:T(8,128)}) custom-call(f32[3,16,16,256]{3,2,1,0:T(8,128)} %vel.1, f32[3,16,16,256]{3,2,1,0:T(8,128)} %met.1), custom_call_target="tpu_custom_call" | custom-call | tf_op jit(solution)/shard_map/pallas_call | solution.py:352
  33.3 0.0 copy-start
  33.3 0.9 %copy-done = f32[16,16,256]{2,1,0:T(8,128)S(1)} copy-done((f32[16,16,256]{2,1,0:T(8,128)S(1)}, f32[16,16,256]{2,1,0:T(8,128)}, u32[]{:S(2)}) %copy-start) | copy-done | bytes 262168
  34.2 0.0 copy-start.1
  34.2 0.7 %copy-done.1 = f32[16,128]{1,0:T(8,128)S(1)} copy-done((f32[16,128]{1,0:T(8,128)S(1)}, f32[16,128]{1,0:T(8,128)}, u32[]{:S(2)}) %copy-start.1) | copy-done | bytes 8216
  34.9 0.8 %shard_map.42 = (f32[16,16,256]{2,1,0:T(8,128)}, f32[16,16]{1,0:T(8,128)}) custom-call(f32[16,16,256]{2,1,0:T(8,128)S(1)} %copy-done, f32[16,128]{1,0:T(8,128)S(1)} %copy-done.1), custom_call_target="tpu_custom_call" | custom-call | tf_op jit(solution)/shard_map/pallas_call | solution.py:377
Async XLA Ops:
  33.3 1.0 %copy-start = (f32[16,16,256]{2,1,0:T(8,128)S(1)}, f32[16,16,256]{2,1,0:T(8,128)}, u32[]{:S(2)}) copy-start(f32[16,16,256]{2,1,0:T(8,128)} %get-tuple-element.4.D) | copy-start | bytes 786436
  34.2 0.7 %copy-start.1 = (f32[16,128]{1,0:T(8,128)S(1)}, f32[16,128]{1,0:T(8,128)}, u32[]{:S(2)}) copy-start(f32[16,128]{1,0:T(8,128)} %get-tuple-element.5.coef) | copy-start | bytes 24580

commit v3 on v2

--- a/solution.py
+++ b/solution.py
@@ -20,7 +20,7 @@
     return {key: 2 * n for n, key in enumerate(order)}
 
 
-def kernel(sizes, vel, met, D, coef_out, V, Gv, G, H, Q, PK, R, LS, PS, sem_in, send, recv, lsend, lrecv, psend, precv):
+def kernel(sizes, vel, met, d_out, coef_out, D, V, Gv, G, H, Q, F, PK, R, LS, PS, sem_in, send, recv, lsend, lrecv, psend, precv):
     NX, NY, NZ = sizes
     nx, ny, nz = vel.shape[1:]
     yr, zr = ny + 8, nz + 128
@@ -216,18 +216,46 @@
         Q[x] = dq
         D[jnp.clip(x - 2, 0, nx - 1)] = dq * mag[0:ny, 0:nz]
         for k, (a, b) in enumerate(pairs):
-            G[k, x] = smooth(smooth(V[a, x] * V[b, x], 0)[0:ny], 1)[:, 0:nz]
-            G[6 + k, x] = smooth(smooth(mag * e[k], 0)[0:ny], 1)[:, 0:nz]
+            put(k, x, V[a, x] * V[b, x])
+            put(6 + k, x, mag * e[k])
         return 0
 
-    lax.fori_loop(2, nx + 2, velocity_plane, 0, unroll=4)
-    lax.fori_loop(3, nx + 1, field_plane, 0)
+    def put(k, x, field):
+        for t in range(zr // 128):
+            tile = field[:, 128 * t : 128 * t + 128]
+            F[k, x, t, 8 : 8 + yr] = tile
+            F[k, x, t, 0:8] = tile[ny:yr]
+
+    first = lane == 0
+    last = lane == 127
+
+    def smooth_plane(x, _):
+        tiles_z = zr // 128
+        for k in range(12):
+            s = []
+            for t in range(tiles_z):
+                mid = F[k, x, t, 8 : 8 + ny]
+                s.append((F[k, x, t, 7 : 7 + ny] + F[k, x, t, 9 : 9 + ny]) + (mid + mid))
+            before = [pltpu.roll(a, 1, 1) for a in s]
+            after = [pltpu.roll(a, 127, 1) for a in s]
+            for t in range(nz // 128):
+                lower = jnp.where(first, before[t - 1], before[t])
+                upper = jnp.where(last, after[t + 1], after[t])
+                G[k, x, :, 128 * t : 128 * t + 128] = (lower + upper) + (s[t] + s[t])
+        return 0
+
+    lax.fori_loop(2, nx + 2, velocity_plane, 0, unroll=8)
+    lax.fori_loop(3, nx + 1, field_plane, 0, unroll=2)
+    lax.fori_loop(3, nx + 1, smooth_plane, 0, unroll=2)
     land(lambda d: d[0] != 0)
     for f in range(6):
         fill_span(f, (0, 1, nx + 2, nx + 3))
-    lax.fori_loop(0, 4, lambda i, c: velocity_plane(jnp.where(i < 2, i, nx + i), c), 0)
-    lax.fori_loop(0, 4, lambda i, c: field_plane(jnp.where(i < 2, i + 1, nx + 4 - i), c), 0)
-
+    lax.fori_loop(0, 4, lambda i, c: velocity_plane(jnp.where(i < 2, i, nx + i), c), 0, unroll=4)
+    lax.fori_loop(0, 4, lambda i, c: field_plane(jnp.where(i < 2, i + 1, nx + 4 - i), c), 0, unroll=2)
+    lax.fori_loop(0, 4, lambda i, c: smooth_plane(jnp.where(i < 2, i + 1, nx + 4 - i), c), 0, unroll=2)
+
+    save = pltpu.make_async_copy(D, d_out, sem_in.at[2])
+    save.start()
     row = lax.broadcasted_iota(jnp.int32, (yr, zr), 0)
     has_lo = jnp.where(iy > 0, 1.0, 0.0)
     has_hi = jnp.where(iy < NY - 1, 1.0, 0.0)
@@ -240,7 +268,7 @@
             H[c, x] = (Gv[c, x - 1] + Gv[c, x + 1] + (mid + mid)) * (row_scale * inside)
         return 0
 
-    lax.fori_loop(1, nx + 3, hat_plane, 0)
+    lax.fori_loop(1, nx + 3, hat_plane, 0, unroll=2)
 
     lane_s = lax.broadcasted_iota(jnp.int32, (ny, 128), 1)
 
@@ -276,7 +304,7 @@
         sums = jnp.where(lane_s == x - 2, num, sums)
         return jnp.where(lane_s == x + 62, den, sums)
 
-    sums = lax.fori_loop(2, nx + 2, line_plane, jnp.zeros((ny, 128), jnp.float32), unroll=2)
+    sums = lax.fori_loop(2, nx + 2, line_plane, jnp.zeros((ny, 128), jnp.float32), unroll=8)
 
     LS[iz] = sums
     def line_copy(o):
@@ -324,6 +352,7 @@
         peak = jnp.maximum(peak, PS[j])
     coef = jnp.minimum(coef, 0.5 * jnp.max(peak, axis=(0, 1), keepdims=True))
     coef_out[...] = coef
+    save.wait()
     for j, (a, b) in enumerate(plane_peers):
         peak_copy(j, a, b, False).wait_send()
     for n, d in enumerate(offsets):
@@ -353,18 +382,20 @@
         functools.partial(kernel, sizes),
         out_shape=(jax.ShapeDtypeStruct((nx, ny, nz), f32), jax.ShapeDtypeStruct((ny, 128), f32)),
         in_specs=[pl.BlockSpec(memory_space=pltpu.HBM)] * 2,
-        out_specs=(pl.BlockSpec(memory_space=pltpu.VMEM),) * 2,
+        out_specs=(pl.BlockSpec(memory_space=pltpu.HBM), pl.BlockSpec(memory_space=pltpu.VMEM)),
         scratch_shapes=[
+            pltpu.VMEM((nx, ny, nz), f32),
             pltpu.VMEM((6, nx + 4, yr, zr), f32),
             pltpu.VMEM((3, nx + 4, yr, zr), f32),
             pltpu.VMEM((12, nx + 4, ny, nz), f32),
             pltpu.VMEM((3, nx + 4, yr, zr), f32),
             pltpu.VMEM((nx + 4, ny, nz), f32),
+            pltpu.VMEM((12, nx + 4, zr // 128, 8 + yr, 128), f32),
             pltpu.VMEM((2, ny, packed), f32),
             pltpu.VMEM((2, 3, 3, ny, packed), f32),
             pltpu.VMEM((NZ, ny, 128), f32),
             pltpu.VMEM((NX * NY, 8, 128), f32),
-            pltpu.SemaphoreType.DMA((2,)),
+            pltpu.SemaphoreType.DMA((3,)),
             pltpu.SemaphoreType.DMA((2 * len(offsets),)),
             pltpu.SemaphoreType.DMA((2 * len(offsets),)),
             pltpu.SemaphoreType.DMA((NZ,)),

time: 35.9 us -> 34.7 us (0.967)
  Pallas kernels: 33.4 us -> 32.2 us
    pallas_call x1, Pallas kernels: 32.6 us -> 31.4 us  [per_device(): pl.pallas_call(functools.partial(kernel, sizes), out_shape=(jax.ShapeDtyp...]
where the time goes in v3:
time: 34.7 us; the launch traced here: 34.5 us
  Pallas kernels  32.2 us (93%)
  local copies, waits for them, and re-layouts  1.64 us (5%)
  between operations  0.65 us (2%)
    pallas_call x1, Pallas kernels, per_device(): pl.pallas_call(functools.partial(kernel, sizes), out_shape=(jax.ShapeDtyp...  31.4 us
    unnamed x4, local copies, waits for them, and re-layouts  1.64 us
    pallas_call x1, Pallas kernels, per_device(): pl.pallas_call(scale_kernel, out_shape=(jax.ShapeDtypeStruct((nx, ny, nz)...  0.81 us

profile of v3, /device:TPU:0, one launch (start us, length us, event | category | flops | bytes accessed | tf_op | source)
XLA Modules:
  0.0 34.5 jit_solution(2184060195593724271)
XLA Ops:
  0.6 31.4 %shard_map.41 = (f32[16,16,256]{2,1,0:T(8,128)}, f32[16,128]{1,0:T(8,128)}) custom-call(f32[3,16,16,256]{3,2,1,0:T(8,128)} %vel.1, f32[3,16,16,256]{3,2,1,0:T(8,128)} %met.1), custom_call_target="tpu_custom_call" | custom-call | tf_op jit(solution)/shard_map/pallas_call | solution.py:381
  32.0 0.0 copy-start
  32.0 0.9 %copy-done = f32[16,16,256]{2,1,0:T(8,128)S(1)} copy-done((f32[16,16,256]{2,1,0:T(8,128)S(1)}, f32[16,16,256]{2,1,0:T(8,128)}, u32[]{:S(2)}) %copy-start) | copy-done | bytes 262168
  33.0 0.0 copy-start.1
  33.0 0.7 %copy-done.1 = f32[16,128]{1,0:T(8,128)S(1)} copy-done((f32[16,128]{1,0:T(8,128)S(1)}, f32[16,128]{1,0:T(8,128)}, u32[]{:S(2)}) %copy-start.1) | copy-done | bytes 8216
  33.7 0.8 %shard_map.42 = (f32[16,16,256]{2,1,0:T(8,128)}, f32[16,16]{1,0:T(8,128)}) custom-call(f32[16,16,256]{2,1,0:T(8,128)S(1)} %copy-done, f32[16,128]{1,0:T(8,128)S(1)} %copy-done.1), custom_call_target="tpu_custom_call" | custom-call | tf_op jit(solution)/shard_map/pallas_call | solution.py:408
Async XLA Ops:
  32.0 1.0 %copy-start = (f32[16,16,256]{2,1,0:T(8,128)S(1)}, f32[16,16,256]{2,1,0:T(8,128)}, u32[]{:S(2)}) copy-start(f32[16,16,256]{2,1,0:T(8,128)} %get-tuple-element.4.D) | copy-start | bytes 786436
  33.0 0.7 %copy-start.1 = (f32[16,128]{1,0:T(8,128)S(1)}, f32[16,128]{1,0:T(8,128)}, u32[]{:S(2)}) copy-start(f32[16,128]{1,0:T(8,128)} %get-tuple-element.5.coef) | copy-start | bytes 24580
